TPU v7x, 32 devices: a whole 2x2x4 slice. The times are simulated.
32 devices in a mesh: row: 4 (over z), col: 8 (over y, x, core).
Axes of the slice: x: 2, y: 2, z: 4, core: 2. Of those that a mesh axis runs over, the one named last changes fastest.
Arguments:
- tokens_in: bfloat16 [8192, 1408], P(('row', 'col')), may hold values from -300 to 300
- ln1_gain: bfloat16 [1408], replicated, may hold values from 0.099609375 to 1.8984375
- ln1_bias: bfloat16 [1408], replicated, may hold values from -3 to 3
- qkv_weight: bfloat16 [1408, 4224], P('row', 'col'), may hold values from -0.8 to 0.8
- qkv_bias: bfloat16 [4224], P('col'), may hold values from -3 to 3
- proj_weight: bfloat16 [1408, 1408], P('col', 'row'), may hold values from -0.15625 to 0.15625
- proj_bias: bfloat16 [1408], replicated, may hold values from -3 to 3
- ln2_gain: bfloat16 [1408], replicated, may hold values from 0.099609375 to 1.8984375
- ln2_bias: bfloat16 [1408], replicated, may hold values from -3 to 3
- fc1_weight: bfloat16 [1408, 6144], P('row', 'col'), may hold values from -0.15625 to 0.15625
- fc1_bias: bfloat16 [6144], P('col'), may hold values from -3 to 3
- fc2_weight: bfloat16 [1408, 6144], P('row', 'col'), may hold values from -0.078125 to 0.078125
- fc2_bias: bfloat16 [1408], replicated, may hold values from -3 to 3
Outputs:
- tokens_out: bfloat16 [8192, 1408], P(('row', 'col'))
All inputs are finite; a program needn't handle non-finite values.
Results may differ from a plain program's by a relative error of at most 0.01.
Values may be sent and summed in bfloat16 or wider, within the bound.
A program may use at most 64 MiB of HBM per device.

v0:
```python
import jax
import jax.numpy as jnp
from jax import lax
from jax.sharding import PartitionSpec as P

HEADS = 16


def norm_local(values, gain, bias):
    mean = jnp.mean(values, axis=-1, keepdims=True)
    centred = values - mean
    var = jnp.mean(centred * centred, axis=-1, keepdims=True)
    return centred * lax.rsqrt(var + 1e-06) * gain.astype(jnp.float32) + bias.astype(jnp.float32)


def attend(qkv, heads):
    length = qkv.shape[0]
    head_size = qkv.shape[1] // (3 * heads)
    parts = qkv.reshape(length, heads, 3, head_size)
    query = parts[:, :, 0]
    keys = parts[:, :, 1]
    values = parts[:, :, 2]
    block = min(512, length)
    blocks = query.reshape(length // block, block, heads, head_size)
    scale = 1.0 / head_size**0.5

    def one_block(qblock):
        scores = (
            jnp.einsum("qhe,khe->hqk", qblock, keys, preferred_element_type=jnp.float32) * scale
        )
        top = jnp.max(scores, axis=-1, keepdims=True)
        expo = jnp.exp(scores - top)
        probs = (expo / jnp.sum(expo, axis=-1, keepdims=True)).astype(jnp.bfloat16)
        mixed = jnp.einsum("hqk,khe->qhe", probs, values, preferred_element_type=jnp.float32)
        return mixed.astype(jnp.bfloat16).reshape(block, heads * head_size)

    return lax.map(one_block, blocks).reshape(length, heads * head_size)


def project_back(left, right):
    return lax.dot_general(
        left, right, (((1,), (1,)), ((), ())), preferred_element_type=jnp.float32
    )


def local(
    tokens_in,
    ln1_gain,
    ln1_bias,
    qkv_weight,
    qkv_bias,
    proj_weight,
    proj_bias,
    ln2_gain,
    ln2_bias,
    fc1_weight,
    fc1_bias,
    fc2_weight,
    fc2_bias,
):
    local_heads = HEADS // lax.axis_size("col")
    own_rows = tokens_in.shape[0]
    inputs = tokens_in.astype(jnp.float32)
    qkv_full = lax.all_gather(qkv_weight, "row", axis=0, tiled=True)
    proj_full = lax.all_gather(proj_weight, "row", axis=1, tiled=True)
    fc1_full = lax.all_gather(fc1_weight, "row", axis=0, tiled=True)
    fc2_full = lax.all_gather(fc2_weight, "row", axis=0, tiled=True)
    qkv_shift = qkv_bias.astype(jnp.float32)
    fc1_shift = fc1_bias.astype(jnp.float32)
    ln1 = norm_local(inputs, ln1_gain, ln1_bias).astype(jnp.bfloat16)
    product = (
        jnp.dot(
            lax.all_gather(ln1, "col", axis=0, tiled=True),
            qkv_full,
            preferred_element_type=jnp.float32,
        )
        + qkv_shift
    )
    qkv = product.astype(jnp.bfloat16)
    attn = attend(qkv, local_heads)
    proj_whole = lax.all_gather(proj_full, "col", axis=0, tiled=True)
    groups = lax.axis_size("col")
    width = proj_whole.shape[0] // groups
    own_heads = lax.all_to_all(attn, "col", split_axis=0, concat_axis=1, tiled=True)
    lefts = own_heads.reshape(own_rows, groups, width)
    rights = proj_whole.reshape(groups, width, proj_whole.shape[1])
    group_parts = jnp.einsum("rgc,gcd->grd", lefts, rights, preferred_element_type=jnp.float32)
    group_parts = lax.optimization_barrier(group_parts.astype(jnp.bfloat16))
    attn_sum = jnp.sum(group_parts.astype(jnp.float32), axis=0)
    resid = inputs + attn_sum + proj_bias.astype(jnp.float32)
    ln2 = norm_local(resid, ln2_gain, ln2_bias).astype(jnp.bfloat16)
    product = (
        jnp.dot(
            lax.all_gather(ln2, "col", axis=0, tiled=True),
            fc1_full,
            preferred_element_type=jnp.float32,
        )
        + fc1_shift
    )
    hidden = jax.nn.gelu(product, approximate=False).astype(jnp.bfloat16)
    mlp_sum = lax.psum_scatter(
        project_back(hidden, fc2_full).astype(jnp.bfloat16), "col", scatter_dimension=0, tiled=True
    ).astype(jnp.float32)
    result = resid + mlp_sum + fc2_bias.astype(jnp.float32)
    return result.astype(jnp.bfloat16)


def solution(mesh):
    in_specs = (
        P(("row", "col"), None),
        P(),
        P(),
        P("row", "col"),
        P("col"),
        P("col", "row"),
        P(),
        P(),
        P(),
        P("row", "col"),
        P("col"),
        P("row", "col"),
        P(),
    )
    out_specs = P(("row", "col"), None)
    return jax.shard_map(local, mesh=mesh, in_specs=in_specs, out_specs=out_specs, check_vma=False)
```

profile of v0, /device:TPU:0, one launch (start us, length us, event | category | flops | bytes accessed | tf_op | source)
XLA Modules:
  0.0 374.7 jit_solution(7904936646565501967)
XLA Ops:
  6.5 0.7 all-gather.19.cloned.1.call-update
  7.3 0.7 convert_element_type.64
  8.0 0.7 convert_element_type.65
  8.7 1.3 convert_reduce_fusion.1
  10.0 1.4 fusion.37
  11.4 2.3 fusion.40
  13.8 0.0 all-gather.11.cloned.1.call-start
  13.8 25.0 %all-gather.1 = bf16[4,352,176]{1,2,0:T(8,128)(2,1)S(1)} all-gather(bf16[1,352,176]{1,2,0:T(8,128)(2,1)} %bitcast.70), channel_id=1, replica_groups=mesh['row'=4,'col'=8] {'row'}, dimensions={0}, use_global_device_ids=true | all-gather | bytes 619520 | tf_op jit(solution)/shard_map/all_gather | solution.py:65
  38.8 0.2 copy.31
  39.0 1.2 reshape.54
  40.2 0.0 all-gather.15.cloned.1.call-start
  40.3 0.5 all-gather.15.cloned.1.call-update
  40.8 0.5 all-gather.17.cloned.1.call-update
  41.4 14.3 %all-gather.19.cloned.1.call-done = bf16[4,352,528]{1,2,0:T(8,128)(2,1)} async-done(((bf16[1,352,528]{1,2,0:T(8,128)(2,1)}), bf16[4,352,528]{1,2,0:T(8,128)(2,1)}) %all-gather.19.cloned.1.call-update) | async-done | bytes 1486864 | tf_op jit(solution)/shard_map/all_gather | solution.py:64
  55.7 2.0 copy.24
  57.8 1.2 reshape.52
  58.9 41.5 %all-gather.9.cloned.1.call-done = bf16[2048,1408]{1,0:T(8,128)(2,1)} async-done(((bf16[256,1408]{1,0:T(8,128)(2,1)}), bf16[2048,1408]{1,0:T(8,128)(2,1)}) %all-gather.9.cloned.1.call-update) | async-done | bytes 5767184 | tf_op jit(solution)/shard_map/all_gather | solution.py:73
  100.5 6.4 %add_convert_fusion = bf16[2048,528]{0,1:T(8,128)(2,1)S(1)} fusion(bf16[2048,1408]{1,0:T(8,128)(2,1)} %all-gather.9.cloned.1.call-done, bf16[1408,528]{0,1:T(8,128)(2,1)S(1)} %reshape.52, f32[528]{0:T(1024)S(1)} %convert_element_type.67), kind=kOutput, calls=%fused_computation.40 | convolution fusion | flops 3047227392 | bytes 9418816 | tf_op jit(solution)/shard_map/dot_general | solution.py:72
  106.9 1.1 slice_bitcast_fusion
  108.0 0.5 reshape_squeeze.3
  108.6 0.1 copy.28
  108.7 48.0 %while.10 = (s32[]{:T(128)}, bf16[4,512,176]{1,2,0:T(8,128)(2,1)S(1)}, bf16[4,512,2,88]{1,3,2,0:T(8,128)(2,1)S(1)}, bf16[2048,2,88]{0,2,1:T(8,128)(2,1)}, bf16[2048,2,88]{0,2,1:T(8,128)(2,1)S(1)}, /*index=5*/s32[]{:T(128)}) while((s32[]{:T(128)}, bf16[4,512,176]{1,2,0:T(8,128)(2,1)S(1)}, bf16[4,512,2,88]{1,3,2,0:T(8,128)(2,1)S(1)}, ...), condition=%wide.region_5.6_spmd, body=%wide.region_2.5_spmd.sunk | while | flops 748775424 | bytes 18948172 | solution.py:37
  108.7 7.1 %fusion.96 = (f32[2,512]{1,0:T(2,128)S(1)}, f32[2,512,2048]{2,1,0:T(8,128)}) fusion(bf16[2048,2,88]{0,2,1:T(8,128)(2,1)} %get-tuple-element.108, bf16[4,512,2,88]{1,3,2,0:T(8,128)(2,1)S(1)} %get-tuple-element.107, s32[]{:T(128)} %get-tuple-element.99), kind=kOutput, calls=%fused_computation.93.clone.1 | convolution fusion | flops 375392256 | bytes 9293828 | tf_op jit(solution)/shard_map/while/body/eval_jaxpr/sub | solution.py:32
  115.9 4.9 %fusion.97 = bf16[2,512,88]{1,2,0:T(8,128)(2,1)S(1)} fusion(bf16[2048,2,88]{0,2,1:T(8,128)(2,1)S(1)} %get-tuple-element.109, f32[2,512,2048]{2,1,0:T(8,128)} %get-tuple-element.91, f32[2,512]{1,0:T(2,128)S(1)} %get-tuple-element.92), kind=kOutput, calls=%fused_computation.7.clone.1 | convolution fusion | flops 373383168 | bytes 9293824 | tf_op jit(solution)/shard_map/while/body/eval_jaxpr/hqk,khe->qhe/dot_general | solution.py:34
  120.8 7.0 %fusion.96 = (f32[2,512]{1,0:T(2,128)S(1)}, f32[2,512,2048]{2,1,0:T(8,128)}) fusion(bf16[2048,2,88]{0,2,1:T(8,128)(2,1)} %get-tuple-element.108, bf16[4,512,2,88]{1,3,2,0:T(8,128)(2,1)S(1)} %get-tuple-element.107, s32[]{:T(128)} %get-tuple-element.99), kind=kOutput, calls=%fused_computation.93.clone.1 | convolution fusion | flops 375392256 | bytes 9293828 | tf_op jit(solution)/shard_map/while/body/eval_jaxpr/sub | solution.py:32
  127.8 4.9 %fusion.97 = bf16[2,512,88]{1,2,0:T(8,128)(2,1)S(1)} fusion(bf16[2048,2,88]{0,2,1:T(8,128)(2,1)S(1)} %get-tuple-element.109, f32[2,512,2048]{2,1,0:T(8,128)} %get-tuple-element.91, f32[2,512]{1,0:T(2,128)S(1)} %get-tuple-element.92), kind=kOutput, calls=%fused_computation.7.clone.1 | convolution fusion | flops 373383168 | bytes 9293824 | tf_op jit(solution)/shard_map/while/body/eval_jaxpr/hqk,khe->qhe/dot_general | solution.py:34
  132.8 7.0 %fusion.96 = (f32[2,512]{1,0:T(2,128)S(1)}, f32[2,512,2048]{2,1,0:T(8,128)}) fusion(bf16[2048,2,88]{0,2,1:T(8,128)(2,1)} %get-tuple-element.108, bf16[4,512,2,88]{1,3,2,0:T(8,128)(2,1)S(1)} %get-tuple-element.107, s32[]{:T(128)} %get-tuple-element.99), kind=kOutput, calls=%fused_computation.93.clone.1 | convolution fusion | flops 375392256 | bytes 9293828 | tf_op jit(solution)/shard_map/while/body/eval_jaxpr/sub | solution.py:32
  139.8 4.9 %fusion.97 = bf16[2,512,88]{1,2,0:T(8,128)(2,1)S(1)} fusion(bf16[2048,2,88]{0,2,1:T(8,128)(2,1)S(1)} %get-tuple-element.109, f32[2,512,2048]{2,1,0:T(8,128)} %get-tuple-element.91, f32[2,512]{1,0:T(2,128)S(1)} %get-tuple-element.92), kind=kOutput, calls=%fused_computation.7.clone.1 | convolution fusion | flops 373383168 | bytes 9293824 | tf_op jit(solution)/shard_map/while/body/eval_jaxpr/hqk,khe->qhe/dot_general | solution.py:34
  144.7 7.1 %fusion.96 = (f32[2,512]{1,0:T(2,128)S(1)}, f32[2,512,2048]{2,1,0:T(8,128)}) fusion(bf16[2048,2,88]{0,2,1:T(8,128)(2,1)} %get-tuple-element.108, bf16[4,512,2,88]{1,3,2,0:T(8,128)(2,1)S(1)} %get-tuple-element.107, s32[]{:T(128)} %get-tuple-element.99), kind=kOutput, calls=%fused_computation.93.clone.1 | convolution fusion | flops 375392256 | bytes 9293828 | tf_op jit(solution)/shard_map/while/body/eval_jaxpr/sub | solution.py:32
  151.8 4.9 %fusion.97 = bf16[2,512,88]{1,2,0:T(8,128)(2,1)S(1)} fusion(bf16[2048,2,88]{0,2,1:T(8,128)(2,1)S(1)} %get-tuple-element.109, f32[2,512,2048]{2,1,0:T(8,128)} %get-tuple-element.91, f32[2,512]{1,0:T(2,128)S(1)} %get-tuple-element.92), kind=kOutput, calls=%fused_computation.7.clone.1 | convolution fusion | flops 373383168 | bytes 9293824 | tf_op jit(solution)/shard_map/while/body/eval_jaxpr/hqk,khe->qhe/dot_general | solution.py:34
  156.7 0.6 copy.29
  157.3 0.2 all_to_all.12
  157.4 1.0 copy.30
  158.4 3.5 all-to-all-start
  162.0 0.2 all-gather.13.cloned.1.call-start
  162.3 11.4 %all-to-all-done = bf16[8,256,176]{1,2,0:T(8,128)(2,1)S(1)} async-done(((bf16[8,256,176]{1,2,0:T(8,128)(2,1)}), bf16[8,256,176]{1,2,0:T(8,128)(2,1)S(1)}, u32[]{:S(2)}, u32[]{:S(2)}) %all-to-all-start) | async-done | bytes 720928 | tf_op jit(solution)/shard_map/all_to_all | solution.py:84
  173.7 4.0 %convolution_convert_fusion.1 = bf16[8,256,1408]{2,1,0:T(8,128)(2,1)S(1)} fusion(bf16[8,176,1408]{2,1,0:T(8,128)(2,1)} %bitcast.66, bf16[8,256,176]{1,2,0:T(8,128)(2,1)S(1)} %all-to-all-done), kind=kOutput, calls=%fused_computation.39 | convolution fusion | flops 1017905152 | bytes 10452992 | tf_op jit(solution)/shard_map/rgc,gcd->grd/dot_general | solution.py:87
  177.8 0.8 convert_reduce_fusion
  178.6 0.3 fusion.73
  178.9 0.4 multiply_reduce_fusion.1
  179.3 1.3 add_convert_fusion.2
  180.6 0.0 reduce-scatter.2.cloned.1.call-start
  180.7 5.5 %all-gather.15.cloned.1.call-done = bf16[1408,768]{1,0:T(8,128)(2,1)} async-done(((bf16[352,768]{1,0:T(8,128)(2,1)}), bf16[1408,768]{1,0:T(8,128)(2,1)}) %all-gather.15.cloned.1.call-update) | async-done | bytes 2162704 | tf_op jit(solution)/shard_map/all_gather | solution.py:66
  186.2 47.0 %all-gather.17.cloned.1.call-done = bf16[1408,768]{1,0:T(8,128)(2,1)} async-done(((bf16[352,768]{1,0:T(8,128)(2,1)}), bf16[1408,768]{1,0:T(8,128)(2,1)}) %all-gather.17.cloned.1.call-update) | async-done | bytes 2162704 | tf_op jit(solution)/shard_map/all_gather | solution.py:67
  233.2 43.7 %all-gather.13.cloned.1.call-done = bf16[2048,1408]{1,0:T(8,128)(2,1)} async-done(((bf16[256,1408]{1,0:T(8,128)(2,1)}), bf16[2048,1408]{1,0:T(8,128)(2,1)}) %all-gather.13.cloned.1.call-update) | async-done | bytes 5767184 | tf_op jit(solution)/shard_map/all_gather | solution.py:94
  276.9 29.4 %convolution_convert_fusion = bf16[2048,1408]{1,0:T(8,128)(2,1)} fusion(bf16[1408,768]{1,0:T(8,128)(2,1)} %all-gather.17.cloned.1.call-done, bf16[2048,1408]{1,0:T(8,128)(2,1)} %all-gather.13.cloned.1.call-done, bf16[1408,768]{1,0:T(8,128)(2,1)} %all-gather.15.cloned.1.call-done, f32[768]{0:T(1024)S(1)} %convert_element_type.75), kind=kOutput, calls=%fused_computation.20 | convolution fusion | flops 8965062656 | bytes 15862784 | tf_op jit(solution)/shard_map/dot_general | solution.py:41
  306.4 59.1 %reduce-scatter.2.cloned.1.call-done = bf16[256,1408]{1,0:T(8,128)(2,1)} async-done(((bf16[2048,1408]{1,0:T(8,128)(2,1)}), bf16[256,1408]{1,0:T(8,128)(2,1)}) %reduce-scatter.2.cloned.1.call-update) | async-done | bytes 720912 | tf_op jit(solution)/shard_map/reduce_scatter | solution.py:101
  365.5 2.3 add_convert_fusion.1
  (39 shorter events, 0.3 us)
Async XLA Ops:
  6.5 34.8 %copy-start.6 = (bf16[528]{0:T(1024)(128)(2,1)S(1)}, bf16[528]{0:T(1024)(128)(2,1)}, u32[]{:S(2)}) copy-start(bf16[528]{0:T(1024)(128)(2,1)} %param.19) | copy-start | bytes 3172
  6.5 49.2 %all-gather.19.cloned.1.call-start = ((), (), s32[]{:S(2)}) async-start(), calls=%async_computation.8 | async-start | bytes 2027520 | tf_op jit(solution)/shard_map/all_gather | solution.py:64
  7.3 93.2 %all-gather.9.cloned.1.call-start = ((), (), s32[]{:S(2)}) async-start(), calls=%async_computation.2 | async-start | bytes 6488064 | tf_op jit(solution)/shard_map/all_gather | solution.py:73
  13.8 148.5 %all-gather.11.cloned.1.call-start = ((), (), s32[]{:S(2)}) async-start(), calls=%async_computation.3 | async-start | bytes 4460544 | tf_op jit(solution)/shard_map/all_gather | solution.py:81
  40.2 146.0 %all-gather.15.cloned.1.call-start = ((), (), s32[]{:S(2)}) async-start(), calls=%async_computation.5 | async-start | bytes 2703360 | tf_op jit(solution)/shard_map/all_gather | solution.py:66
  40.8 192.4 %all-gather.17.cloned.1.call-start = ((), (), s32[]{:S(2)}) async-start(), calls=%async_computation.6 | async-start | bytes 2703360 | tf_op jit(solution)/shard_map/all_gather | solution.py:67
  106.9 1.8 copy-start.1
  108.7 53.5 %copy-start.2 = (bf16[1408]{0:T(1024)(128)(2,1)S(1)}, bf16[1408]{0:T(1024)(128)(2,1)}, u32[]{:S(2)}) copy-start(bf16[1408]{0:T(1024)(128)(2,1)} %param.21) | copy-start | bytes 8452
  108.7 53.5 %copy-start.3 = (bf16[1408]{0:T(1024)(128)(2,1)S(1)}, bf16[1408]{0:T(1024)(128)(2,1)}, u32[]{:S(2)}) copy-start(bf16[1408]{0:T(1024)(128)(2,1)} %param.22) | copy-start | bytes 8452
  108.7 53.5 %copy-start.4 = (bf16[1408]{0:T(1024)(128)(2,1)S(1)}, bf16[1408]{0:T(1024)(128)(2,1)}, u32[]{:S(2)}) copy-start(bf16[1408]{0:T(1024)(128)(2,1)} %param.23) | copy-start | bytes 8452
  158.4 15.3 %all-to-all-start = ((bf16[8,256,176]{1,2,0:T(8,128)(2,1)}), bf16[8,256,176]{1,2,0:T(8,128)(2,1)S(1)}, u32[]{:S(2)}, u32[]{:S(2)}) async-start(bf16[8,256,176]{1,2,0:T(8,128)(2,1)} %copy.30), calls=%async_computation | async-start | bytes 1441792 | tf_op jit(solution)/shard_map/all_to_all | solution.py:84
  162.0 114.9 %all-gather.13.cloned.1.call-start = ((), (), s32[]{:S(2)}) async-start(), calls=%async_computation.4 | async-start | bytes 6488064 | tf_op jit(solution)/shard_map/all_gather | solution.py:94
  173.7 4.9 %copy-start = (bf16[256,1408]{1,0:T(8,128)(2,1)S(1)}, bf16[256,1408]{1,0:T(8,128)(2,1)}, u32[]{:S(2)}) copy-start(bf16[256,1408]{1,0:T(8,128)(2,1)} %param.15) | copy-start | bytes 2162692
  177.8 2.9 copy-start.7
  180.6 184.9 %reduce-scatter.2.cloned.1.call-start = ((), (), s32[]{:S(2)}) async-start(), calls=%async_computation.7 | async-start | bytes 6488064 | tf_op jit(solution)/shard_map/reduce_scatter | solution.py:101
  180.7 125.7 %copy-start.5 = (bf16[1408]{0:T(1024)(128)(2,1)S(1)}, bf16[1408]{0:T(1024)(128)(2,1)}, u32[]{:S(2)}) copy-start(bf16[1408]{0:T(1024)(128)(2,1)} %param.27) | copy-start | bytes 8452
Sparse Core Ops, SparseCore 0:
  8.9 46.7 all-gather.18
  57.6 42.8 all-gather.8
  102.4 35.6 all-gather.10
  139.4 46.7 all-gather.14
  187.6 45.5 all-gather.16
  234.9 41.9 all-gather.12
  306.5 58.9 reduce-scatter.1
where the time goes:
time: 375 us
  waiting for transfers between devices  225 us (60%)
  matrix products  87.7 us (23%)
  blocking collectives  25 us (7%)
  between operations  13.8 us (4%)
  other arithmetic  11.5 us (3%)
  local copies, waits for them, and re-layouts  8.19 us (2%)
  starting transfers between devices  3.97 us (1%)
    reduce_scatter x1, waiting for transfers between devices, local(): lax.psum_scatter(project_back(hidden, fc2_full).astype(jnp.bfloat16), 'co...  59.1 us
    all_gather x1, waiting for transfers between devices, local(): fc2_full = lax.all_gather(fc2_weight, 'row', axis=0, tiled=True)  47 us
    all_gather x1, waiting for transfers between devices, local(): lax.all_gather(ln2, 'col', axis=0, tiled=True)  43.7 us
    all_gather x1, waiting for transfers between devices, local(): lax.all_gather(ln1, 'col', axis=0, tiled=True)  41.5 us
    dot_general x1, matrix products, project_back(): lax.dot_general(left, right, (((1,), (1,)), ((), ())), preferred_element_...  29.4 us
    sub x4, matrix products, one_block(): expo = jnp.exp(scores - top)  28.3 us
    all_gather x1, blocking collectives, local(): proj_full = lax.all_gather(proj_weight, 'row', axis=1, tiled=True)  25 us
    dot_general x4, matrix products, one_block(): jnp.einsum('hqk,khe->qhe', probs, values, preferred_element_type=jnp.floa...  19.5 us
  transfers between devices with their start and end apart: 8, of which 7 were waited for; matrix products, arithmetic and copies ran while one was open for 20% of the time, Pallas kernels for 0%

commit v1 on v0

--- a/solution.py
+++ b/solution.py
@@ -64,7 +64,12 @@
     qkv_full = lax.all_gather(qkv_weight, "row", axis=0, tiled=True)
     proj_full = lax.all_gather(proj_weight, "row", axis=1, tiled=True)
     fc1_full = lax.all_gather(fc1_weight, "row", axis=0, tiled=True)
-    fc2_full = lax.all_gather(fc2_weight, "row", axis=0, tiled=True)
+    ring = [fc2_weight]
+    for hop in range(3):
+        ring.append(lax.ppermute(ring[-1], "row", [(dev, (dev + 1) % 4) for dev in range(4)]))
+    fc2_full = jnp.roll(
+        jnp.concatenate(ring[::-1], axis=0), (lax.axis_index("row") + 1) * ring[0].shape[0], axis=0
+    )
     qkv_shift = qkv_bias.astype(jnp.float32)
     fc1_shift = fc1_bias.astype(jnp.float32)
     ln1 = norm_local(inputs, ln1_gain, ln1_bias).astype(jnp.bfloat16)

time: 375 us -> 338 us (0.901)
  waiting for transfers between devices: 225 us -> 173 us
  local copies, waits for them, and re-layouts: 8.19 us -> 20.1 us
    all_gather x1 -> x0, waiting for transfers between devices: 47 us -> none  [local(): fc2_full = lax.all_gather(fc2_weight, 'row', axis=0, tiled=True)]
    ppermute x0 -> x3, waiting for transfers between devices: none -> 44.9 us  [local(): lax.ppermute(ring[-1], 'row', [(dev, (dev + 1) % 4) for dev in range(4)])]
    all_gather x1, waiting for transfers between devices: 43.7 us -> 0.01 us  [local(): lax.all_gather(ln2, 'col', axis=0, tiled=True)]
    unnamed x18 -> x27, local copies, waits for them, and re-layouts: 2.39 us -> 13.4 us
    all_gather x1, waiting for transfers between devices: 5.53 us -> 0.01 us  [local(): fc1_full = lax.all_gather(fc1_weight, 'row', axis=0, tiled=True)]
  transfers between devices with their start and end apart: 8 -> 10, of which waited for: 7 -> 7; matrix products, arithmetic and copies ran while one was open for 20% -> 26% of each run, Pallas kernels for 0% -> 0%
where the time goes in v1:
time: 338 us; the launch traced here: 336 us
  waiting for transfers between devices  173 us (51%)
  matrix products  87.9 us (26%)
  blocking collectives  25 us (7%)
  local copies, waits for them, and re-layouts  20.1 us (6%)
  between operations  13.7 us (4%)
  other arithmetic  11.5 us (3%)
  starting transfers between devices  5.48 us (2%)
    reduce_scatter x1, waiting for transfers between devices, local(): lax.psum_scatter(project_back(hidden, fc2_full).astype(jnp.bfloat16), 'co...  58.6 us
    ppermute x3, waiting for transfers between devices, local(): lax.ppermute(ring[-1], 'row', [(dev, (dev + 1) % 4) for dev in range(4)])  44.9 us
    all_gather x1, waiting for transfers between devices, local(): lax.all_gather(ln1, 'col', axis=0, tiled=True)  41.5 us
    dot_general x1, matrix products, project_back(): lax.dot_general(left, right, (((1,), (1,)), ((), ())), preferred_element_...  29.8 us
    sub x4, matrix products, one_block(): expo = jnp.exp(scores - top)  28.3 us
    all_gather x1, blocking collectives, local(): proj_full = lax.all_gather(proj_weight, 'row', axis=1, tiled=True)  25 us
    dot_general x4, matrix products, one_block(): jnp.einsum('hqk,khe->qhe', probs, values, preferred_element_type=jnp.floa...  19.5 us
    all_gather x1, waiting for transfers between devices, local(): qkv_full = lax.all_gather(qkv_weight, 'row', axis=0, tiled=True)  14.9 us
  transfers between devices with their start and end apart: 10, of which 7 were waited for; matrix products, arithmetic and copies ran while one was open for 26% of the time, Pallas kernels for 0%

profile of v1, /device:TPU:0, one launch (start us, length us, event | category | flops | bytes accessed | tf_op | source)
XLA Modules:
  0.0 336.4 jit_solution(13639198028117858087)
XLA Ops:
  6.5 0.7 all-gather.16.cloned.1.call-update
  7.3 0.7 convert_element_type.64
  8.0 0.7 convert_element_type.65
  8.7 1.3 convert_reduce_fusion.1
  10.0 1.4 fusion.38
  11.4 2.3 fusion.41
  13.8 25.0 %all-gather.1 = bf16[4,352,176]{1,2,0:T(8,128)(2,1)S(1)} all-gather(bf16[1,352,176]{1,2,0:T(8,128)(2,1)} %bitcast.69), channel_id=1, replica_groups=mesh['row'=4,'col'=8] {'row'}, dimensions={0}, use_global_device_ids=true | all-gather | bytes 619520 | tf_op jit(solution)/shard_map/all_gather | solution.py:65
  39.0 1.2 reshape.54
  40.3 0.5 all-gather.14.cloned.1.call-update
  40.9 14.9 %all-gather.16.cloned.1.call-done = bf16[4,352,528]{1,2,0:T(8,128)(2,1)} async-done(((bf16[1,352,528]{1,2,0:T(8,128)(2,1)}), bf16[4,352,528]{1,2,0:T(8,128)(2,1)}) %all-gather.16.cloned.1.call-update) | async-done | bytes 1486864 | tf_op jit(solution)/shard_map/all_gather | solution.py:64
  55.7 2.0 copy.24
  57.8 1.2 reshape.52
  58.9 41.5 %all-gather.8.cloned.1.call-done = bf16[2048,1408]{1,0:T(8,128)(2,1)} async-done(((bf16[256,1408]{1,0:T(8,128)(2,1)}), bf16[2048,1408]{1,0:T(8,128)(2,1)}) %all-gather.8.cloned.1.call-update) | async-done | bytes 5767184 | tf_op jit(solution)/shard_map/all_gather | solution.py:78
  100.5 6.4 %add_convert_fusion = bf16[2048,528]{0,1:T(8,128)(2,1)S(1)} fusion(bf16[2048,1408]{1,0:T(8,128)(2,1)} %all-gather.8.cloned.1.call-done, bf16[1408,528]{0,1:T(8,128)(2,1)S(1)} %reshape.52, f32[528]{0:T(1024)S(1)} %convert_element_type.67), kind=kOutput, calls=%fused_computation.40 | convolution fusion | flops 3047227392 | bytes 9418816 | tf_op jit(solution)/shard_map/dot_general | solution.py:77
  106.9 1.1 slice_bitcast_fusion
  108.1 0.5 reshape_squeeze.3
  108.7 47.9 %while.10 = (s32[]{:T(128)}, bf16[4,512,176]{1,2,0:T(8,128)(2,1)S(1)}, bf16[4,512,2,88]{1,3,2,0:T(8,128)(2,1)S(1)}, bf16[2048,2,88]{0,2,1:T(8,128)(2,1)}, bf16[2048,2,88]{0,2,1:T(8,128)(2,1)S(1)}, /*index=5*/s32[]{:T(128)}) while((s32[]{:T(128)}, bf16[4,512,176]{1,2,0:T(8,128)(2,1)S(1)}, bf16[4,512,2,88]{1,3,2,0:T(8,128)(2,1)S(1)}, ...), condition=%wide.region_5.6_spmd, body=%wide.region_2.5_spmd.sunk | while | flops 748775424 | bytes 18948172 | solution.py:37
  108.7 7.1 %fusion.97 = (f32[2,512]{1,0:T(2,128)S(1)}, f32[2,512,2048]{2,1,0:T(8,128)}) fusion(bf16[2048,2,88]{0,2,1:T(8,128)(2,1)} %get-tuple-element.108, bf16[4,512,2,88]{1,3,2,0:T(8,128)(2,1)S(1)} %get-tuple-element.107, s32[]{:T(128)} %get-tuple-element.99), kind=kOutput, calls=%fused_computation.103.clone.1 | convolution fusion | flops 375392256 | bytes 9293828 | tf_op jit(solution)/shard_map/while/body/eval_jaxpr/sub | solution.py:32
  115.8 4.9 %fusion.98 = bf16[2,512,88]{1,2,0:T(8,128)(2,1)S(1)} fusion(bf16[2048,2,88]{0,2,1:T(8,128)(2,1)S(1)} %get-tuple-element.109, f32[2,512,2048]{2,1,0:T(8,128)} %get-tuple-element.91, f32[2,512]{1,0:T(2,128)S(1)} %get-tuple-element.92), kind=kOutput, calls=%fused_computation.7.clone.1 | convolution fusion | flops 373383168 | bytes 9293824 | tf_op jit(solution)/shard_map/while/body/eval_jaxpr/hqk,khe->qhe/dot_general | solution.py:34
  120.7 7.0 %fusion.97 = (f32[2,512]{1,0:T(2,128)S(1)}, f32[2,512,2048]{2,1,0:T(8,128)}) fusion(bf16[2048,2,88]{0,2,1:T(8,128)(2,1)} %get-tuple-element.108, bf16[4,512,2,88]{1,3,2,0:T(8,128)(2,1)S(1)} %get-tuple-element.107, s32[]{:T(128)} %get-tuple-element.99), kind=kOutput, calls=%fused_computation.103.clone.1 | convolution fusion | flops 375392256 | bytes 9293828 | tf_op jit(solution)/shard_map/while/body/eval_jaxpr/sub | solution.py:32
  127.8 4.9 %fusion.98 = bf16[2,512,88]{1,2,0:T(8,128)(2,1)S(1)} fusion(bf16[2048,2,88]{0,2,1:T(8,128)(2,1)S(1)} %get-tuple-element.109, f32[2,512,2048]{2,1,0:T(8,128)} %get-tuple-element.91, f32[2,512]{1,0:T(2,128)S(1)} %get-tuple-element.92), kind=kOutput, calls=%fused_computation.7.clone.1 | convolution fusion | flops 373383168 | bytes 9293824 | tf_op jit(solution)/shard_map/while/body/eval_jaxpr/hqk,khe->qhe/dot_general | solution.py:34
  132.8 7.0 %fusion.97 = (f32[2,512]{1,0:T(2,128)S(1)}, f32[2,512,2048]{2,1,0:T(8,128)}) fusion(bf16[2048,2,88]{0,2,1:T(8,128)(2,1)} %get-tuple-element.108, bf16[4,512,2,88]{1,3,2,0:T(8,128)(2,1)S(1)} %get-tuple-element.107, s32[]{:T(128)} %get-tuple-element.99), kind=kOutput, calls=%fused_computation.103.clone.1 | convolution fusion | flops 375392256 | bytes 9293828 | tf_op jit(solution)/shard_map/while/body/eval_jaxpr/sub | solution.py:32
  139.8 4.9 %fusion.98 = bf16[2,512,88]{1,2,0:T(8,128)(2,1)S(1)} fusion(bf16[2048,2,88]{0,2,1:T(8,128)(2,1)S(1)} %get-tuple-element.109, f32[2,512,2048]{2,1,0:T(8,128)} %get-tuple-element.91, f32[2,512]{1,0:T(2,128)S(1)} %get-tuple-element.92), kind=kOutput, calls=%fused_computation.7.clone.1 | convolution fusion | flops 373383168 | bytes 9293824 | tf_op jit(solution)/shard_map/while/body/eval_jaxpr/hqk,khe->qhe/dot_general | solution.py:34
  144.7 7.1 %fusion.97 = (f32[2,512]{1,0:T(2,128)S(1)}, f32[2,512,2048]{2,1,0:T(8,128)}) fusion(bf16[2048,2,88]{0,2,1:T(8,128)(2,1)} %get-tuple-element.108, bf16[4,512,2,88]{1,3,2,0:T(8,128)(2,1)S(1)} %get-tuple-element.107, s32[]{:T(128)} %get-tuple-element.99), kind=kOutput, calls=%fused_computation.103.clone.1 | convolution fusion | flops 375392256 | bytes 9293828 | tf_op jit(solution)/shard_map/while/body/eval_jaxpr/sub | solution.py:32
  151.8 4.9 %fusion.98 = bf16[2,512,88]{1,2,0:T(8,128)(2,1)S(1)} fusion(bf16[2048,2,88]{0,2,1:T(8,128)(2,1)S(1)} %get-tuple-element.109, f32[2,512,2048]{2,1,0:T(8,128)} %get-tuple-element.91, f32[2,512]{1,0:T(2,128)S(1)} %get-tuple-element.92), kind=kOutput, calls=%fused_computation.7.clone.1 | convolution fusion | flops 373383168 | bytes 9293824 | tf_op jit(solution)/shard_map/while/body/eval_jaxpr/hqk,khe->qhe/dot_general | solution.py:34
  156.7 0.6 copy.29
  157.4 1.0 copy.30
  158.4 3.5 %all-to-all-start = ((bf16[8,256,176]{1,2,0:T(8,128)(2,1)}), bf16[8,256,176]{1,2,0:T(8,128)(2,1)S(1)}, u32[]{:S(2)}, u32[]{:S(2)}) async-start(bf16[8,256,176]{1,2,0:T(8,128)(2,1)} %copy.30), calls=%async_computation | async-start | bytes 1441792 | tf_op jit(solution)/shard_map/all_to_all | solution.py:89
  162.3 11.4 %all-to-all-done = bf16[8,256,176]{1,2,0:T(8,128)(2,1)S(1)} async-done(((bf16[8,256,176]{1,2,0:T(8,128)(2,1)}), bf16[8,256,176]{1,2,0:T(8,128)(2,1)S(1)}, u32[]{:S(2)}, u32[]{:S(2)}) %all-to-all-start) | async-done | bytes 720928 | tf_op jit(solution)/shard_map/all_to_all | solution.py:89
  173.8 4.0 %convolution_convert_fusion.1 = bf16[8,256,1408]{2,1,0:T(8,128)(2,1)S(1)} fusion(bf16[8,176,1408]{2,1,0:T(8,128)(2,1)} %bitcast.65, bf16[8,256,176]{1,2,0:T(8,128)(2,1)S(1)} %all-to-all-done), kind=kOutput, calls=%fused_computation.39 | convolution fusion | flops 1017905152 | bytes 10452992 | tf_op jit(solution)/shard_map/rgc,gcd->grd/dot_general | solution.py:92
  177.7 0.8 convert_reduce_fusion
  179.5 1.3 add_convert_fusion.2
  180.9 1.5 collective-permute-start
  182.4 15.7 %collective-permute-done = bf16[352,768]{1,0:T(8,128)(2,1)S(1)} collective-permute-done((bf16[352,768]{1,0:T(8,128)(2,1)S(1)}, bf16[352,768]{1,0:T(8,128)(2,1)S(1)}, u32[]{:S(2)}, u32[]{:S(2)}) %collective-permute-start) | collective-permute-done | bytes 540704 | tf_op jit(solution)/shard_map/ppermute | solution.py:69
  198.1 14.9 %collective-permute-done.1 = bf16[352,768]{1,0:T(8,128)(2,1)} collective-permute-done((bf16[352,768]{1,0:T(8,128)(2,1)S(1)}, bf16[352,768]{1,0:T(8,128)(2,1)}, u32[]{:S(2)}, u32[]{:S(2)}) %collective-permute-start.1) | collective-permute-done | bytes 540704 | tf_op jit(solution)/shard_map/ppermute | solution.py:69
  213.1 14.3 %collective-permute-done.2 = bf16[352,768]{1,0:T(8,128)(2,1)} collective-permute-done((bf16[352,768]{1,0:T(8,128)(2,1)}, bf16[352,768]{1,0:T(8,128)(2,1)}, u32[]{:S(2)}, u32[]{:S(2)}) %collective-permute-start.2) | collective-permute-done | bytes 540704 | tf_op jit(solution)/shard_map/ppermute | solution.py:69
  227.3 1.9 constant_dynamic-update-slice_fusion.7
  229.2 1.9 constant_dynamic-update-slice_fusion.6
  231.1 0.9 constant_dynamic-update-slice_fusion.5
  231.9 0.8 constant_dynamic-update-slice_fusion.4
  232.8 1.9 constant_dynamic-update-slice_fusion.3
  234.7 1.9 constant_dynamic-update-slice_fusion.2
  236.6 0.8 constant_dynamic-update-slice_fusion.1
  237.4 0.9 constant_dynamic-update-slice_fusion
  238.3 29.8 %convolution_convert_fusion = bf16[2048,1408]{1,0:T(8,128)(2,1)} fusion(bf16[2048,1408]{1,0:T(8,128)(2,1)} %all-gather.12.cloned.1.call-done, bf16[1408,768]{1,0:T(8,128)(2,1)} %all-gather.14.cloned.1.call-done, f32[768]{0:T(1024)S(1)} %convert_element_type.75, bf16[2816,768]{1,0:T(8,128)(2,1)} %constant_dynamic-update-slice_fusion, s32[]{:T(128)S(6)} %select_n.14), kind=kOutput, calls=%fused_computation.20 | convolution fusion | flops 8965062656 | bytes 15862788 | tf_op jit(solution)/shard_map/dot_general | solution.py:41
  268.1 0.7 copy-done.6
  268.7 58.6 %reduce-scatter.2.cloned.1.call-done = bf16[256,1408]{1,0:T(8,128)(2,1)} async-done(((bf16[2048,1408]{1,0:T(8,128)(2,1)}), bf16[256,1408]{1,0:T(8,128)(2,1)}) %reduce-scatter.2.cloned.1.call-update) | async-done | bytes 720912 | tf_op jit(solution)/shard_map/reduce_scatter | solution.py:106
  327.3 2.3 add_convert_fusion.1
  (52 shorter events, 2.1 us)
Async XLA Ops:
  6.5 34.3 %copy-start.7 = (bf16[528]{0:T(1024)(128)(2,1)S(1)}, bf16[528]{0:T(1024)(128)(2,1)}, u32[]{:S(2)}) copy-start(bf16[528]{0:T(1024)(128)(2,1)} %param.19) | copy-start | bytes 3172
  6.5 49.2 %all-gather.16.cloned.1.call-start = ((), (), s32[]{:S(2)}) async-start(), calls=%async_computation.7 | async-start | bytes 2027520 | tf_op jit(solution)/shard_map/all_gather | solution.py:64
  7.3 93.2 %all-gather.8.cloned.1.call-start = ((), (), s32[]{:S(2)}) async-start(), calls=%async_computation.2 | async-start | bytes 6488064 | tf_op jit(solution)/shard_map/all_gather | solution.py:78
  13.8 148.5 %all-gather.10.cloned.1.call-start = ((), (), s32[]{:S(2)}) async-start(), calls=%async_computation.3 | async-start | bytes 4460544 | tf_op jit(solution)/shard_map/all_gather | solution.py:86
  40.2 198.0 %all-gather.14.cloned.1.call-start = ((), (), s32[]{:S(2)}) async-start(), calls=%async_computation.5 | async-start | bytes 2703360 | tf_op jit(solution)/shard_map/all_gather | solution.py:66
  106.9 1.8 copy-start.2
  156.7 5.6 %copy-start.3 = (bf16[1408]{0:T(1024)(128)(2,1)S(1)}, bf16[1408]{0:T(1024)(128)(2,1)}, u32[]{:S(2)}) copy-start(bf16[1408]{0:T(1024)(128)(2,1)} %param.21) | copy-start | bytes 8452
  156.7 5.6 %copy-start.4 = (bf16[1408]{0:T(1024)(128)(2,1)S(1)}, bf16[1408]{0:T(1024)(128)(2,1)}, u32[]{:S(2)}) copy-start(bf16[1408]{0:T(1024)(128)(2,1)} %param.22) | copy-start | bytes 8452
  156.7 5.6 %copy-start.5 = (bf16[1408]{0:T(1024)(128)(2,1)S(1)}, bf16[1408]{0:T(1024)(128)(2,1)}, u32[]{:S(2)}) copy-start(bf16[1408]{0:T(1024)(128)(2,1)} %param.23) | copy-start | bytes 8452
  158.4 15.3 %all-to-all-start = ((bf16[8,256,176]{1,2,0:T(8,128)(2,1)}), bf16[8,256,176]{1,2,0:T(8,128)(2,1)S(1)}, u32[]{:S(2)}, u32[]{:S(2)}) async-start(bf16[8,256,176]{1,2,0:T(8,128)(2,1)} %copy.30), calls=%async_computation | async-start | bytes 1441792 | tf_op jit(solution)/shard_map/all_to_all | solution.py:89
  162.0 76.3 %all-gather.12.cloned.1.call-start = ((), (), s32[]{:S(2)}) async-start(), calls=%async_computation.4 | async-start | bytes 6488064 | tf_op jit(solution)/shard_map/all_gather | solution.py:99
  177.7 1.1 copy-start
  178.8 2.0 copy-start.1
  178.8 34.2 %copy-start.8 = (bf16[768]{0:T(1024)(128)(2,1)S(1)}, bf16[768]{0:T(1024)(128)(2,1)}, u32[]{:S(2)}) copy-start(bf16[768]{0:T(1024)(128)(2,1)} %param.25) | copy-start | bytes 4612
  180.8 146.5 %reduce-scatter.2.cloned.1.call-start = ((), (), s32[]{:S(2)}) async-start(), calls=%async_computation.6 | async-start | bytes 6488064 | tf_op jit(solution)/shard_map/reduce_scatter | solution.py:106
  180.9 17.3 %collective-permute-start = (bf16[352,768]{1,0:T(8,128)(2,1)S(1)}, bf16[352,768]{1,0:T(8,128)(2,1)S(1)}, u32[]{:S(2)}, u32[]{:S(2)}) collective-permute-start(bf16[352,768]{1,0:T(8,128)(2,1)S(1)} %copy-done.1), channel_id=1, source_target_pairs={{0,8},{8,16},{16,24},{24,0},{1,9},{9,17},{17,25},{25,1},{2,10},{10... | collective-permute-start | bytes 1622024 | tf_op jit(solution)/shard_map/ppermute | solution.py:69
  198.1 14.9 %collective-permute-start.1 = (bf16[352,768]{1,0:T(8,128)(2,1)S(1)}, bf16[352,768]{1,0:T(8,128)(2,1)}, u32[]{:S(2)}, u32[]{:S(2)}) collective-permute-start(bf16[352,768]{1,0:T(8,128)(2,1)S(1)} %collective-permute-done), channel_id=1, source_target_pairs={{0,8},{8,16},{16,24},{24,0},{1,9},{9,17},{17,25},{25,1},{2,10},{10... | collective-permute-start | bytes 1622024 | tf_op jit(solution)/shard_map/ppermute | solution.py:69
  213.0 14.3 %collective-permute-start.2 = (bf16[352,768]{1,0:T(8,128)(2,1)}, bf16[352,768]{1,0:T(8,128)(2,1)}, u32[]{:S(2)}, u32[]{:S(2)}) collective-permute-start(bf16[352,768]{1,0:T(8,128)(2,1)} %collective-permute-done.1), channel_id=1, source_target_pairs={{0,8},{8,16},{16,24},{24,0},{1,9},{9,17},{17,25},{25,1},{2,10},{10... | collective-permute-start | bytes 1622024 | tf_op jit(solution)/shard_map/ppermute | solution.py:69
  268.0 0.7 copy-start.6
Sparse Core Ops, SparseCore 0:
  8.9 46.7 all-gather.15
  57.6 42.8 all-gather.7
  102.4 35.6 all-gather.9
  139.4 48.9 all-gather.13
  190.1 42.7 all-gather.11
  268.2 59.0 reduce-scatter.1
